TPU v7x, 256 devices: a whole 4x4x8 slice. The times are simulated.
256 devices in a mesh: depth: 2 (over z_hi), row: 8 (over y, core), col: 16 (over x, z_lo).
Axes of the slice: x: 4, y: 4, z: 8 (z_hi: 2, z_lo: 4; z = z_hi * 4 + z_lo), core: 2. Of those that a mesh axis runs over, the one named last changes fastest.
Arguments:
- q_slab: float32 [6144, 1024], P('col', ('depth', 'row')), may hold values from -6 to 6
- triangle: float32 [1024, 1024], P(None, 'depth'), as said below
- panel_q: float32 [32768, 1024], P('row', ('depth', 'col')), may hold values from -0.1875 to 0.1875
Outputs:
- slab_out: float32 [6144, 32768], P('col', 'row')
Inputs may be any that keep to these rules, and one draw needn't show every extreme that they name: triangle is zero below its diagonal; its diagonal lies in 0.5 to 1.5.
All inputs are finite; a program needn't handle non-finite values.
Results may differ from a plain program's by a relative error of at most 0.000071.
Values sent between devices are 32-bit elements; how exact they have to be, the bound alone decides.
A program may use at most 64 MiB of HBM per device.

v0:
```python
import jax
import jax.numpy as jnp
from jax import lax
from jax.sharding import Mesh
from jax.sharding import PartitionSpec as P

COL = ("col_0", "col_1")
DEPTH_COL = ("depth", "col_0", "col_1")


def in_order(blocks, dim):
    dims = list(blocks.shape[1:])
    dims[dim] *= blocks.shape[0]
    return jnp.moveaxis(blocks, 0, dim).reshape(dims)


def sent_to_all(value, axis):
    copies = jnp.broadcast_to(value, (lax.axis_size(axis), *value.shape))
    return lax.all_to_all(copies, axis, split_axis=0, concat_axis=0, tiled=True)


def collect(value, axis, dim):
    return in_order(sent_to_all(value, axis), dim)


def gather_axes(value, axes, dim):
    filled = value
    for number in range(len(axes) - 1, -1, -1):
        filled = lax.all_gather(filled, axes[number], axis=dim, tiled=True)
    return filled


def per_device(q_slab, triangle, panel_q):
    rows = q_slab.shape[0]
    left = jnp.dot(
        lax.all_gather(q_slab, ("depth", "row"), axis=1, tiled=True),
        triangle,
        precision=lax.Precision.HIGHEST,
        preferred_element_type=jnp.float32,
    )
    narrow = panel_q.shape[1]
    columns = lax.axis_size(COL)
    mixed = lax.all_to_all(panel_q, "depth", split_axis=0, concat_axis=1, tiled=True)
    left_all = collect(left, "depth", 1)
    grid = left_all.reshape(rows, 2, columns, narrow)
    piece = gather_axes(mixed, COL, 1)
    count = piece.shape[1] // (2 * narrow)
    pieces = piece.reshape(piece.shape[0], count, 2, narrow)
    partial_out = jnp.einsum(
        "sdnw,rndw->sr",
        grid,
        pieces,
        precision=lax.Precision.HIGHEST,
        preferred_element_type=jnp.float32,
    )
    return collect(partial_out, "depth", 1)


def solution(mesh):
    torus = Mesh(
        mesh.devices.reshape(mesh.shape["depth"], mesh.shape["row"], 4, 4),
        ("depth", "row", "col_0", "col_1"),
    )
    in_specs = (P(COL, ("depth", "row")), P(None, "depth"), P("row", DEPTH_COL))
    out_specs = P(COL, "row")
    return jax.shard_map(
        per_device, mesh=torus, in_specs=in_specs, out_specs=out_specs, check_vma=False
    )
```

profile of v0, /device:TPU:6, one launch (start us, length us, event | category | flops | bytes accessed | tf_op | source)
XLA Modules:
  0.0 406.0 jit_solution(865121534383447310)
XLA Ops:
  6.5 0.0 copy-start
  6.5 0.0 all-gather.6.cloned.1.call-start
  6.5 1.2 copy.26
  7.8 24.5 %all_to_all.29 = f32[2,2048,32]{1,2,0:T(8,128)} all-to-all(f32[2,2048,32]{1,2,0:T(8,128)S(1)} %bitcast.25), channel_id=1, replica_groups=mesh['depth'=2,'row'=8,'col_0'=4,'col_1'=4] {'depth'}, dimensions={0} | all-to-all | bytes 1048576 | tf_op jit(solution)/shard_map/all_to_all | solution.py:43
  32.2 0.0 all-gather.6.cloned.1.call-update
  32.3 0.0 all-gather.4.cloned.1.call-start
  32.3 0.7 all-gather.4.cloned.1.call-update
  33.0 0.0 all-gather.8.cloned.1.call-start
  33.1 47.9 %all-gather.6.cloned.1.call-done = f32[2048,256]{0,1:T(8,128)} async-done(((f32[2048,64]{0,1:T(8,128)}), f32[2048,256]{0,1:T(8,128)}) %all-gather.6.cloned.1.call-update) | async-done | bytes 2097168 | tf_op jit(solution)/shard_map/all_gather | solution.py:29
  81.0 0.0 all-gather.8.cloned.1.call-update
  81.0 61.5 %all-gather.4.cloned.1.call-done = f32[384,1024]{0,1:T(8,128)} async-done(((f32[384,64]{0,1:T(8,128)}), f32[384,1024]{0,1:T(8,128)}) %all-gather.4.cloned.1.call-update) | async-done | bytes 1572880 | tf_op jit(solution)/shard_map/all_gather | solution.py:36
  142.5 0.0 copy-done
  142.5 4.9 %fusion.5 = f32[384,512]{0,1:T(8,128)S(1)} fusion(f32[384,1024]{0,1:T(8,128)} %all-gather.4.cloned.1.call-done, f32[1024,512]{1,0:T(8,128)S(1)} %copy-done), kind=kOutput, calls=%fused_computation.4 | convolution fusion | flops 2415919104 | bytes 4456448 | tf_op jit(solution)/shard_map/dot_general | solution.py:35
  147.3 0.1 broadcast_in_dim.6
  147.5 42.3 %all_to_all.30 = f32[2,384,512]{1,2,0:T(8,128)} all-to-all(f32[2,384,512]{1,2,0:T(8,128)S(1)} %broadcast_in_dim.6), channel_id=1, replica_groups=mesh['depth'=2,'row'=8,'col_0'=4,'col_1'=4] {'depth'}, dimensions={0} | all-to-all | bytes 3145728 | tf_op jit(solution)/shard_map/all_to_all | solution.py:19
  189.7 34.9 %all-gather.8.cloned.1.call-done = f32[2048,1024]{0,1:T(8,128)} async-done(((f32[2048,256]{0,1:T(8,128)}), f32[2048,1024]{0,1:T(8,128)}) %all-gather.8.cloned.1.call-update) | async-done | bytes 8388624 | tf_op jit(solution)/shard_map/all_gather | solution.py:29
  224.6 13.1 %fusion.2 = f32[384,2048]{1,0:T(8,128)S(1)} fusion(f32[384,2,16,32]{0,3,2,1:T(8,128)} %bitcast.23, f32[2048,16,2,32]{0,3,2,1:T(8,128)} %bitcast.22), kind=kOutput, calls=%fused_computation.2 | convolution fusion | flops 9663676416 | bytes 13107200 | tf_op jit(solution)/shard_map/sdnw,rndw->sr/dot_general | solution.py:49
  237.8 0.8 broadcast_in_dim.7
  238.6 147.8 %all_to_all.31 = f32[2,384,2048]{2,1,0:T(8,128)} all-to-all(f32[2,384,2048]{2,1,0:T(8,128)S(1)} %broadcast_in_dim.7), channel_id=1, replica_groups=mesh['depth'=2,'row'=8,'col_0'=4,'col_1'=4] {'depth'}, dimensions={0} | all-to-all | bytes 12582912 | tf_op jit(solution)/shard_map/all_to_all | solution.py:19
  386.3 6.6 %copy.16 = f32[2,384,2048]{1,2,0:T(8,128)} copy(f32[2,384,2048]{2,1,0:T(8,128)} %all_to_all.31) | data formatting | bytes 12582912 | tf_op jit(solution)/shard_map/all_to_all | solution.py:19
  392.9 6.6 %copy.17 = f32[384,4096]{1,0:T(8,128)} copy(f32[384,4096]{0,1:T(8,128)} %bitcast.21) | data formatting | bytes 12582912 | tf_op jit(solution)/shard_map/reshape | solution.py:14
Async XLA Ops:
  6.5 135.9 %copy-start = (f32[1024,512]{1,0:T(8,128)S(1)}, f32[1024,512]{1,0:T(8,128)}, u32[]{:S(2)}) copy-start(f32[1024,512]{1,0:T(8,128)} %param.4) | copy-start | bytes 6291460
  6.5 74.4 %all-gather.6.cloned.1.call-start = ((), (), s32[]{:S(2)}) async-start(), calls=%async_computation.4 | async-start | bytes 2621440 | tf_op jit(solution)/shard_map/all_gather | solution.py:29
  32.3 110.2 %all-gather.4.cloned.1.call-start = ((), (), s32[]{:S(2)}) async-start(), calls=%async_computation.3 | async-start | bytes 1671168 | tf_op jit(solution)/shard_map/all_gather | solution.py:36
  33.0 191.6 %all-gather.8.cloned.1.call-start = ((), (), s32[]{:S(2)}) async-start(), calls=%async_computation.5 | async-start | bytes 10485760 | tf_op jit(solution)/shard_map/all_gather | solution.py:29
Sparse Core Ops, SparseCore 0:
  32.4 48.5 all-gather.5
  83.7 58.7 all-gather.3
  144.3 80.3 all-gather.7
where the time goes:
time: 407 us; the launch traced here: 406 us
  blocking collectives  215 us (53%)
  waiting for transfers between devices  145 us (36%)
  matrix products  18 us (4%)
  local copies, waits for them, and re-layouts  15.2 us (4%)
  between operations  13.1 us (3%)
    all_to_all x2, blocking collectives, sent_to_all(): return lax.all_to_all(copies, axis, split_axis=0, concat_axis=0, tiled=True)  190 us
    all_gather x2, waiting for transfers between devices, gather_axes(): filled = lax.all_gather(filled, axes[number], axis=dim, tiled=True)  82.8 us
    all_gather x1, waiting for transfers between devices, per_device(): lax.all_gather(q_slab, ('depth', 'row'), axis=1, tiled=True)  61.5 us
    all_to_all x1, blocking collectives, per_device(): lax.all_to_all(panel_q, 'depth', split_axis=0, concat_axis=1, tiled=True)  24.5 us
    dot_general x1, matrix products, per_device(): jnp.einsum('sdnw,rndw->sr', grid, pieces, precision=lax.Precision.HIGHEST...  13.1 us
  transfers between devices with their start and end apart: 3, of which 3 were waited for; matrix products, arithmetic and copies ran while one was open for 1% of the time, Pallas kernels for 0%

commit v1 on v0

v1 whole, which is shorter than its diff:
```python
import functools

import jax
import jax.numpy as jnp
from jax import lax
from jax.experimental import pallas as pl
from jax.experimental.pallas import tpu as pltpu
from jax.sharding import Mesh
from jax.sharding import PartitionSpec as P

AXES = ("depth", "y", "core", "x", "zl")
MESH = pl.DeviceIdType.MESH
F32, BF16 = jnp.float32, jnp.bfloat16


def split(value):
    high = value.astype(BF16)
    return high, (value - high.astype(F32)).astype(BF16)


def dot(a, b):
    return jnp.dot(a, b, preferred_element_type=F32)


def kernel(dims, unit, q_ref, t_ref, p_ref, out_ref,
           qbuf, qrow, lf, lhi, llo, gat, phi, plo, obuf,
           q_send, q_recv, e_send, e_recv, e_own, z_send, z_recv,
           d_send, d_recv, lx_send, lx_recv, y_send, y_recv,
           c_send, c_recv, o_own, o_send, o_recv):
    nd, ny, nc, nx, nzl = dims
    nz = nd * nzl
    nr = ny * nc
    nb = nd * nr
    d, y, core, x, zl = (lax.axis_index(a) for a in AXES)
    z = d * nzl + zl
    rk = y * nc + core
    me_b = d * nr + rk
    chunks = gat.shape[0]
    piece = lf.shape[3]
    half = lf.shape[4]
    k_full = nd * half
    rows = nr * piece
    qk = q_ref.shape[1]

    def dev(**over):
        return tuple(over.get(a, v) for a, v in zip(AXES, (d, y, core, x, zl)))

    def at_z(pos):
        pos = lax.rem(pos + nz, nz)
        return lax.div(pos, nzl), lax.rem(pos, nzl)

    def at_b(pos):
        pos = lax.rem(pos, nb)
        dd, r = lax.div(pos, nr), lax.rem(pos, nr)
        return dd, lax.div(r, nc), lax.rem(r, nc), r

    def remote(src, dst, send, recv, to):
        return pltpu.make_async_remote_copy(
            src_ref=src, dst_ref=dst, send_sem=send, recv_sem=recv,
            device_id=to, device_id_type=MESH)

    def role_of(pos, j):
        return lax.rem(pos + j, 2)

    barrier = pltpu.get_barrier_semaphore()
    for o in range(1, nb):
        dd, yy, cc, _ = at_b(me_b + o)
        pl.semaphore_signal(barrier, inc=1, device_id=dev(depth=dd, y=yy, core=cc), device_id_type=MESH)
    for o in range(1, nx):
        pl.semaphore_signal(barrier, inc=1, device_id=dev(x=lax.rem(x + o, nx)), device_id_type=MESH)
    for o in (1, nz - 1):
        dd, zz = at_z(z + o)
        pl.semaphore_signal(barrier, inc=1, device_id=dev(depth=dd, zl=zz), device_id_type=MESH)
    pl.semaphore_wait(barrier, nb - 1 + nx - 1 + 2)

    def q_copy(o):
        dd, yy, cc, r = at_b(me_b + o)
        src = q_ref.at[pl.ds(pl.multiple_of(r * piece, 8), piece)]
        return remote(src, qbuf.at[me_b], q_send.at[o], q_recv.at[o], dev(depth=dd, y=yy, core=cc))

    def q_arrival(o):
        src = lax.rem(me_b + nb - o, nb)
        dd, yy, cc, _ = at_b(src)
        return remote(qbuf.at[src], qbuf.at[src], q_send.at[o], q_recv.at[o], dev(depth=dd, y=yy, core=cc))

    def q_start(o, _):
        q_copy(o).start()
        return 0

    lax.fori_loop(1, nb, q_start, 0)

    def e_copy(j, o):
        to = lax.rem(x + o, nx)
        block = 2 * j + role_of(to, j)
        src = p_ref.at[:, pl.ds(pl.multiple_of(block * unit, unit), unit)]
        return remote(src, gat.at[j, d, x, zl], e_send.at[j, o], e_recv.at[j, o], dev(x=to))

    def e_arrival(j, o):
        src = lax.rem(x + nx - o, nx)
        ref = gat.at[j, d, src, zl]
        return remote(ref, ref, e_send.at[j, o], e_recv.at[j, o], dev(x=src))

    def e_local(j):
        block = 2 * j + role_of(x, j)
        src = p_ref.at[:, pl.ds(pl.multiple_of(block * unit, unit), unit)]
        return pltpu.make_async_copy(src, gat.at[j, d, x, zl], e_own.at[j])

    def e_start(j, _):
        e_local(j).start()
        for o in range(1, nx):
            e_copy(j, o).start()
        return 0

    lax.fori_loop(0, chunks, e_start, 0)

    nlong, nshort = nz // 2, (nz - 1) // 2

    def z_copy(j, hop, far):
        sign = 1 - 2 * lax.rem(j, 2)
        step = sign if far else -sign
        index = hop - 1 if far else nlong + hop - 1
        dd, zz = at_z(z - step * (hop - 1))
        to_d, to_z = at_z(z + step)
        ref = gat.at[j, dd, :, zz]
        return remote(ref, ref, z_send.at[j, index], z_recv.at[j, index], dev(depth=to_d, zl=to_z))

    def z_arrival(j, hop, far):
        sign = 1 - 2 * lax.rem(j, 2)
        step = sign if far else -sign
        index = hop - 1 if far else nlong + hop - 1
        dd, zz = at_z(z - step * hop)
        from_d, from_z = at_z(z - step)
        ref = gat.at[j, dd, :, zz]
        return remote(ref, ref, z_send.at[j, index], z_recv.at[j, index], dev(depth=from_d, zl=from_z))

    def hop(j, h):
        if h == 1:
            e_local(j).wait()
            for o in range(1, nx):
                e_arrival(j, o).wait_recv()
        for far, count in ((True, nlong), (False, nshort)):
            if 2 <= h <= count + 1:
                z_arrival(j, h - 1, far).wait_recv()
            if h <= count:
                z_copy(j, h, far).start()

    def left_piece():
        qbuf[me_b] = q_ref[pl.ds(pl.multiple_of(rk * piece, 8), piece), :]

        def q_wait(o, _):
            q_arrival(o).wait_recv()
            return 0

        lax.fori_loop(1, nb, q_wait, 0)
        for b in range(nb):
            qrow[:, b * qk:(b + 1) * qk] = qbuf[b]
        qh, ql = split(qrow[...])
        th, tl = split(t_ref[...])
        lf[d, x, rk] = dot(qh, th) + dot(qh, tl) + dot(ql, th)

    def depth_copy(dd):
        ref = lf.at[dd, x, rk]
        return remote(ref, ref, d_send.at[0], d_recv.at[0], dev(depth=1 - d))

    def lx_copy(o):
        ref = lf.at[:, x, rk]
        return remote(ref, ref, lx_send.at[o], lx_recv.at[o], dev(x=lax.rem(x + o, nx)))

    def lx_arrival(o):
        src = lax.rem(x + nx - o, nx)
        ref = lf.at[:, src, rk]
        return remote(ref, ref, lx_send.at[o], lx_recv.at[o], dev(x=src))

    ylong, yshort = ny // 2, (ny - 1) // 2

    def y_index(h, far):
        return h - 1 if far else ylong + h - 1

    def y_step(xs, far):
        sign = 1 - 2 * lax.rem(xs, 2)
        return sign if far else -sign

    def y_copy(xs, h, far):
        step = y_step(xs, far)
        owner = lax.rem(y - step * (h - 1) + ny, ny)
        ref = lf.at[:, xs, owner * nc + core]
        i = y_index(h, far)
        return remote(ref, ref, y_send.at[xs, i], y_recv.at[xs, i], dev(y=lax.rem(y + step + ny, ny)))

    def y_arrival(xs, h, far):
        step = y_step(xs, far)
        owner = lax.rem(y - step * h + ny, ny)
        ref = lf.at[:, xs, owner * nc + core]
        i = y_index(h, far)
        return remote(ref, ref, y_send.at[xs, i], y_recv.at[xs, i], dev(y=lax.rem(y - step + ny, ny)))

    def c_copy(xs, h, far, arriving=False):
        owner = lax.rem(y - y_step(xs, far) * h + ny, ny)
        i = 0 if h == 0 else 1 + y_index(h, far)
        ref = lf.at[:, xs, owner * nc + (1 - core if arriving else core)]
        return remote(ref, ref, c_send.at[xs, i], c_recv.at[xs, i], dev(core=1 - core))

    def y_first(xs):
        c_copy(xs, 0, True).start()
        for far, count in ((True, ylong), (False, yshort)):
            if count >= 1:
                y_copy(xs, 1, far).start()

    def y_later(xs, h):
        for far, count in ((True, ylong), (False, yshort)):
            if 1 <= h - 1 <= count:
                y_arrival(xs, h - 1, far).wait_recv()
                if h <= count:
                    y_copy(xs, h, far).start()
                c_copy(xs, h - 1, far).start()

    def y_blocks():
        return [(0, True)] + [(h, True) for h in range(1, ylong + 1)] + [(h, False) for h in range(1, yshort + 1)]

    def each_xs(body):
        def step(o, _):
            body(lax.rem(x + o, nx))
            return 0
        lax.fori_loop(0, nx, step, 0)

    def left_ready(xs):
        for h, far in y_blocks():
            c_copy(xs, h, far, arriving=True).wait_recv()
        for b in range(nd):
            high, low = split(lf[b, xs].reshape(rows, half))
            lhi[xs, :, b * half:(b + 1) * half] = high
            llo[xs, :, b * half:(b + 1) * half] = low

    def partner_of(j):
        return lax.rem(x + 1 - 2 * role_of(x, j) + nx, nx)

    def own_copy(j):
        block = 2 * j + role_of(x, j)
        dst = out_ref.at[:, pl.ds(pl.multiple_of(block * unit, unit), unit)]
        return pltpu.make_async_copy(obuf.at[j, 0], dst, o_own.at[j])

    def ship_copy(j, arriving=False):
        block = 2 * j + (1 - role_of(x, j) if arriving else role_of(x, j))
        dst = out_ref.at[:, pl.ds(pl.multiple_of(block * unit, unit), unit)]
        return remote(obuf.at[j, 1], dst, o_send.at[j], o_recv.at[j], dev(x=partner_of(j)))

    def compute(j):
        if nlong > 3:
            z_arrival(j, nlong, True).wait_recv()
        high, low = split(gat[j].reshape(k_full, unit))
        phi[...] = high
        plo[...] = low

        def product(xs):
            return (dot(lhi[xs], phi[...]) + dot(lhi[xs], plo[...])) + dot(llo[xs], phi[...])

        def side(s, _):
            xs = jnp.where(s == 0, partner_of(j), x)
            obuf[j, 1 - s] = product(xs)
            return 0

        obuf[j, 1] = product(partner_of(j))
        ship_copy(j).start()
        obuf[j, 0] = product(x)
        own_copy(j).start()

    hop(0, 1)
    left_piece()
    depth_copy(d).start()
    hop(0, 2)
    hop(1, 1)
    depth_copy(1 - d).wait_recv()
    for o in range(1, nx):
        lx_copy(o).start()
    y_first(x)
    hop(0, 3)
    hop(1, 2)
    for o in range(1, nx):
        lx_arrival(o).wait_recv()
        y_first(lax.rem(x + nx - o, nx))
    hop(0, 4)
    hop(1, 3)
    hop(2, 1)
    for h in range(2, ylong + 1):
        each_xs(functools.partial(y_later, h=h))
    hop(1, 4)
    hop(2, 2)
    each_xs(functools.partial(y_later, h=ylong + 1))
    each_xs(left_ready)

    def body(i, _):
        @pl.when(i - 1 < chunks)
        def _():
            hop(i - 1, 3)

        @pl.when(i < chunks)
        def _():
            hop(i, 1)

        compute(i - 3)

        @pl.when(i - 1 < chunks)
        def _():
            hop(i - 1, 4)

        @pl.when(i < chunks)
        def _():
            hop(i, 2)

        return 0

    lax.fori_loop(3, chunks + 3, body, 0)

    def finish(j, _):
        own_copy(j).wait()
        ship_copy(j).wait_send()
        ship_copy(j, arriving=True).wait_recv()
        for o in range(1, nx):
            e_copy(j, o).wait_send()
        for h in range(1, nlong + 1):
            z_copy(j, h, True).wait_send()
        for h in range(1, nshort + 1):
            z_copy(j, h, False).wait_send()
        return 0

    lax.fori_loop(0, chunks, finish, 0)

    def q_finish(o, _):
        q_copy(o).wait_send()
        return 0

    lax.fori_loop(1, nb, q_finish, 0)
    depth_copy(d).wait_send()
    for o in range(1, nx):
        lx_copy(o).wait_send()

    def y_finish(xs):
        for h, far in y_blocks():
            c_copy(xs, h, far).wait_send()
            if h:
                y_copy(xs, h, far).wait_send()

    each_xs(y_finish)


def per_device(dims, unit, q_slab, triangle, panel_q):
    nd, ny, nc, nx, nzl = dims
    nz, nr, nb = nd * nzl, ny * nc, nd * ny * nc
    rows, qk = q_slab.shape
    k_full, half = triangle.shape
    out_cols, narrow = panel_q.shape
    chunks = out_cols // (2 * unit)
    dma = pltpu.SemaphoreType.DMA
    vmem = pl.BlockSpec(memory_space=pltpu.VMEM)
    return pl.pallas_call(
        functools.partial(kernel, dims, unit),
        out_shape=jax.ShapeDtypeStruct((rows, out_cols), F32),
        in_specs=[vmem] * 3,
        out_specs=pl.BlockSpec(memory_space=pl.ANY),
        scratch_shapes=[
            pltpu.VMEM((nb, rows // nr, qk), F32),
            pltpu.VMEM((rows // nr, k_full), F32),
            pltpu.VMEM((nd, nx, nr, rows // nr, half), F32),
            pltpu.VMEM((nx, rows, k_full), BF16),
            pltpu.VMEM((nx, rows, k_full), BF16),
            pltpu.VMEM((chunks, nd, nx, nzl, narrow, unit), F32),
            pltpu.VMEM((k_full, unit), BF16),
            pltpu.VMEM((k_full, unit), BF16),
            pltpu.VMEM((chunks, 2, rows, unit), F32),
            dma((nb,)), dma((nb,)),
            dma((chunks, nx)), dma((chunks, nx)), dma((chunks,)),
            dma((chunks, nz)), dma((chunks, nz)),
            dma((1,)), dma((1,)),
            dma((nx,)), dma((nx,)),
            dma((nx, ny)), dma((nx, ny)),
            dma((nx, ny)), dma((nx, ny)),
            dma((chunks,)), dma((chunks,)), dma((chunks,)),
        ],
        compiler_params=pltpu.CompilerParams(
            collective_id=0, has_side_effects=True, vmem_limit_bytes=60 * 1024 * 1024
        ),
    )(q_slab, triangle, panel_q.T)


def build(mesh, dims, unit):
    torus = Mesh(mesh.devices.reshape(dims), AXES)
    slab = ("x", "zl")
    row = ("y", "core")
    in_specs = (P(slab, ("depth",) + row), P(None, "depth"), P(row, ("depth",) + slab))
    return jax.shard_map(
        functools.partial(per_device, dims, unit),
        mesh=torus, in_specs=in_specs, out_specs=P(slab, row), check_vma=False)


def solution(mesh):
    return build(mesh, (mesh.shape["depth"], 4, 2, 4, 4), 256)
```

time: 407 us -> 159 us (0.39)
  blocking collectives: 215 us -> 0 us
  Pallas kernels: 0 us -> 150 us
  waiting for transfers between devices: 145 us -> 0 us
  matrix products: 18 us -> 0 us
  between operations: 13.1 us -> 0.01 us
  local copies, waits for them, and re-layouts: 15.2 us -> 7.9 us
    all_to_all x3 -> x0, blocking collectives: 215 us -> none  [the longest x2 190 us: sent_to_all(): return lax.all_to_all(copies, axis, split_axis=0, concat_axis=0, tiled=True)]
    pallas_call x0 -> x1, Pallas kernels: none -> 150 us  [per_device(): pl.pallas_call(functools.partial(kernel, dims, unit), out_shape=jax.Shape...]
    all_gather x3 -> x0, waiting for transfers between devices: 144 us -> none  [the longest x2 82.8 us: gather_axes(): filled = lax.all_gather(filled, axes[number], axis=dim, tiled=True)]
    dot_general x2 -> x0, matrix products: 18 us -> none  [the longest x1 13.1 us: per_device(): jnp.einsum('sdnw,rndw->sr', grid, pieces, precision=lax.Precision.HIGHEST...]
    unnamed x2, local copies, waits for them, and re-layouts: 0.01 us -> 7.9 us
    all_to_all x2 -> x0, local copies, waits for them, and re-layouts: 7.78 us -> none  [the longest x1 6.56 us: sent_to_all(): return lax.all_to_all(copies, axis, split_axis=0, concat_axis=0, tiled=True)]
    reshape x1 -> x0, local copies, waits for them, and re-layouts: 6.56 us -> none  [in_order(): return jnp.moveaxis(blocks, 0, dim).reshape(dims)]
  transfers between devices with their start and end apart: 3 -> 0, of which waited for: 3 -> 0; matrix products, arithmetic and copies ran while one was open for 1% -> 0% of each run, Pallas kernels for 0% -> 0%
where the time goes in v1:
time: 159 us; the launch traced here: 158 us
  Pallas kernels  150 us (94%)
  local copies, waits for them, and re-layouts  7.9 us (5%)
    pallas_call x1, Pallas kernels, per_device(): pl.pallas_call(functools.partial(kernel, dims, unit), out_shape=jax.Shape...  150 us
    unnamed x2, local copies, waits for them, and re-layouts  7.9 us

profile of v1, /device:TPU:6, one launch (start us, length us, event | category | flops | bytes accessed | tf_op | source)
XLA Modules:
  0.0 157.5 jit_solution(3593151191737023806)
XLA Ops:
  0.0 1.7 %copy.4.q_ref = f32[384,64]{1,0:T(8,128)} copy(f32[384,64]{0,1:T(8,128)} %param.3) | data formatting | bytes 196608 | tf_op args[0]
  1.7 149.6 %shard_map.37 = f32[384,4096]{1,0:T(8,128)} custom-call(f32[384,64]{1,0:T(8,128)} %copy.4.q_ref, f32[1024,512]{1,0:T(8,128)} %t_ref.1, f32[32,4096]{1,0:T(8,128)} %bitcast.1), custom_call_target="tpu_custom_call" | custom-call | tf_op jit(solution)/shard_map/pallas_call | solution.py:355
  151.3 6.2 %copy.6 = f32[384,4096]{1,0:T(8,128)} copy(f32[384,4096]{1,0:T(8,128)} %shard_map.37) | data formatting | bytes 12582912

commit v2 on v1

v2 whole, which is shorter than its diff:
```python
import functools

import jax
import jax.numpy as jnp
from jax import lax
from jax.experimental import pallas as pl
from jax.experimental.pallas import tpu as pltpu
from jax.sharding import Mesh
from jax.sharding import PartitionSpec as P

AXES = ("depth", "y", "core", "x", "zl")
MESH = pl.DeviceIdType.MESH
F32, BF16 = jnp.float32, jnp.bfloat16


def split(value):
    high = value.astype(BF16)
    return high, (value - high.astype(F32)).astype(BF16)


def dot(a, b):
    return jnp.dot(a, b, preferred_element_type=F32)


def kernel(dims, unit, groups, q_ref, t_hbm, p_hbm, out_ref,
           qs, t_ref, p_ref, qbuf, qrow, lf, lhi, llo, gat, phi, plo, obuf, in_sem,
           q_send, q_recv, e_send, e_recv, e_own, z_send, z_recv,
           d_send, d_recv, lx_send, lx_recv, y_send, y_recv,
           c_send, c_recv, o_own, o_send, o_recv):
    wide, pairs = groups
    nd, ny, nc, nx, nzl = dims
    nz = nd * nzl
    nr = ny * nc
    nb = nd * nr
    d, y, core, x, zl = (lax.axis_index(a) for a in AXES)
    z = d * nzl + zl
    rk = y * nc + core
    me_b = d * nr + rk
    chunks = 2 * pairs
    ahead = 6
    piece = lf.shape[3]
    half = lf.shape[4]
    k_full = nd * half
    rows = nr * piece
    qk = qs.shape[1]

    def dev(**over):
        return tuple(over.get(a, v) for a, v in zip(AXES, (d, y, core, x, zl)))

    def at_z(pos):
        pos = lax.rem(pos + nz, nz)
        return lax.div(pos, nzl), lax.rem(pos, nzl)

    def at_b(pos):
        pos = lax.rem(pos, nb)
        dd, r = lax.div(pos, nr), lax.rem(pos, nr)
        return dd, lax.div(r, nc), lax.rem(r, nc), r

    def remote(src, dst, send, recv, to):
        return pltpu.make_async_remote_copy(
            src_ref=src, dst_ref=dst, send_sem=send, recv_sem=recv,
            device_id=to, device_id_type=MESH)

    def base(m):
        return 2 * m + 2 * jnp.minimum(m, wide)

    def share(pos, m):
        return jnp.where(m < wide, pos, lax.rem(pos + m, 2))

    def partner_of(m):
        return lax.rem(x + 1 - 2 * lax.rem(x + m, 2) + nx, nx)

    t_load = pltpu.make_async_copy(t_hbm, t_ref, in_sem.at[0])
    p_load = pltpu.make_async_copy(p_hbm, p_ref, in_sem.at[1])
    p_load.start()
    t_load.start()

    barrier = pltpu.get_barrier_semaphore()

    def greet(o, _):
        dd, yy, cc, _ = at_b(me_b + o)
        pl.semaphore_signal(barrier, inc=1, device_id=dev(depth=dd, y=yy, core=cc), device_id_type=MESH)
        return 0

    lax.fori_loop(1, nb, greet, 0)
    for o in range(1, nx):
        pl.semaphore_signal(barrier, inc=1, device_id=dev(x=lax.rem(x + o, nx)), device_id_type=MESH)
    for o in (1, nz - 1):
        dd, zz = at_z(z + o)
        pl.semaphore_signal(barrier, inc=1, device_id=dev(depth=dd, zl=zz), device_id_type=MESH)
    qs[...] = q_ref[...].T
    qbuf[me_b] = qs[pl.ds(pl.multiple_of(rk * piece, 8), piece), :]
    p_load.wait()
    pl.semaphore_wait(barrier, nb - 1 + nx - 1 + 2)

    def q_copy(o):
        dd, yy, cc, r = at_b(me_b + o)
        src = qs.at[pl.ds(pl.multiple_of(r * piece, 8), piece)]
        return remote(src, qbuf.at[me_b], q_send.at[o], q_recv.at[o], dev(depth=dd, y=yy, core=cc))

    def q_arrival(o):
        src = lax.rem(me_b + nb - o, nb)
        dd, yy, cc, _ = at_b(src)
        return remote(qbuf.at[src], qbuf.at[src], q_send.at[o], q_recv.at[o], dev(depth=dd, y=yy, core=cc))

    def e_rows(j, pos):
        m = lax.div(j, 2)
        start = (2 * (base(m) + share(pos, m)) + lax.rem(j, 2)) * unit
        return p_ref.at[:, pl.ds(pl.multiple_of(start, unit), unit)]

    def e_copy(j, o):
        to = lax.rem(x + o, nx)
        return remote(e_rows(j, to), gat.at[j, d, x, zl], e_send.at[j, o], e_recv.at[j, o], dev(x=to))

    def e_arrival(j, o):
        src = lax.rem(x + nx - o, nx)
        ref = gat.at[j, d, src, zl]
        return remote(ref, ref, e_send.at[j, o], e_recv.at[j, o], dev(x=src))

    def e_local(j):
        return pltpu.make_async_copy(e_rows(j, x), gat.at[j, d, x, zl], e_own.at[j])

    def e_start(j):
        for o in (1, nx - 1, 2):
            e_copy(j, o).start()
        e_local(j).start()

    def e_step(j, _):
        e_start(j)
        return 0

    def q_step(o, _):
        q_copy(o).start()
        return 0

    e_start(0)
    lax.fori_loop(1, nb, q_step, 0)
    lax.fori_loop(1, min(ahead, chunks), e_step, 0)

    nlong, nshort = nz // 2, (nz - 1) // 2

    def z_parts(j, hop, far, arriving):
        sign = 1 - 2 * lax.rem(j, 2)
        step = sign if far else -sign
        index = hop - 1 if far else nlong + hop - 1
        dd, zz = at_z(z - step * (hop if arriving else hop - 1))
        to_d, to_z = at_z(z - step if arriving else z + step)
        ref = gat.at[j, dd, :, zz]
        return remote(ref, ref, z_send.at[j, index], z_recv.at[j, index], dev(depth=to_d, zl=to_z))

    def z_copy(j, hop, far):
        return z_parts(j, hop, far, False)

    def z_arrival(j, hop, far):
        return z_parts(j, hop, far, True)

    def hop(j, h):
        if h == 1:
            e_local(j).wait()
            for o in (1, nx - 1, 2):
                e_arrival(j, o).wait_recv()
        for far, count in ((True, nlong), (False, nshort)):
            if 2 <= h <= count + 1:
                z_arrival(j, h - 1, far).wait_recv()
            if h <= count:
                z_copy(j, h, far).start()

    def slot(t):
        for h in range(nlong + 1, 0, -1):
            if isinstance(t, int):
                if 0 <= t - h < chunks:
                    hop(t - h, h)
            else:
                pl.when((t - h >= 0) & (t - h < chunks))(functools.partial(hop, t - h, h))
        nxt = t + ahead - 1
        if isinstance(t, int):
            if nxt < chunks:
                e_start(nxt)
        else:
            pl.when(nxt < chunks)(functools.partial(e_start, nxt))

    ylong, yshort = ny // 2, (ny - 1) // 2
    ways = [(h, True) for h in range(1, ylong + 1)] + [(h, False) for h in range(1, yshort + 1)]

    def columns_of(e):
        return d if e == 0 else 1 - d

    def left_piece():
        def q_wait(o, _):
            q_arrival(o).wait_recv()
            return 0

        lax.fori_loop(1, nb, q_wait, 0)
        for b in range(nb):
            qrow[:, b * qk:(b + 1) * qk] = qbuf[b]
        t_load.wait()
        qh, ql = split(qrow[...])
        th, tl = split(t_ref[...])
        lf[d, x, rk] = dot(qh, th) + dot(qh, tl) + dot(ql, th)

    def depth_copy(e):
        ref = lf.at[columns_of(e), x, rk]
        return remote(ref, ref, d_send.at[0], d_recv.at[0], dev(depth=1 - d))

    def lx_copy(o, e):
        ref = lf.at[columns_of(e), x, rk]
        return remote(ref, ref, lx_send.at[o, e], lx_recv.at[o, e], dev(x=lax.rem(x + o, nx)))

    def lx_arrival(o, e):
        src = lax.rem(x + nx - o, nx)
        ref = lf.at[columns_of(e), src, rk]
        return remote(ref, ref, lx_send.at[o, e], lx_recv.at[o, e], dev(x=src))

    def y_index(h, far):
        return h - 1 if far else ylong + h - 1

    def y_step(xs, far):
        sign = 1 - 2 * lax.rem(xs, 2)
        return sign if far else -sign

    def y_parts(xs, e, h, far, arriving):
        step = y_step(xs, far)
        owner = lax.rem(y - step * (h if arriving else h - 1) + ny, ny)
        to = lax.rem((y - step if arriving else y + step) + ny, ny)
        ref = lf.at[columns_of(e), xs, owner * nc + core]
        i = y_index(h, far)
        return remote(ref, ref, y_send.at[xs, e, i], y_recv.at[xs, e, i], dev(y=to))

    def c_copy(xs, e, h, far, arriving=False):
        owner = lax.rem(y - y_step(xs, far) * h + ny, ny)
        i = 0 if h == 0 else 1 + y_index(h, far)
        ref = lf.at[columns_of(e), xs, owner * nc + (1 - core if arriving else core)]
        return remote(ref, ref, c_send.at[xs, e, i], c_recv.at[xs, e, i], dev(core=1 - core))

    def y_first(xs, e):
        for h, far in ways:
            if h == 1:
                y_parts(xs, e, 1, far, False).start()
        c_copy(xs, e, 0, True).start()

    def y_later(xs, e, h):
        for far, count in ((True, ylong), (False, yshort)):
            if 1 <= h - 1 <= count:
                y_parts(xs, e, h - 1, far, True).wait_recv()
                if h <= count:
                    y_parts(xs, e, h, far, False).start()
                c_copy(xs, e, h - 1, far).start()

    def each_xs(work):
        def step(o, _):
            work(lax.rem(x + o, nx))
            return 0
        lax.fori_loop(0, nx, step, 0)

    def left_ready(xs):
        for h, far in [(0, True)] + ways:
            for e in range(2):
                c_copy(xs, e, h, far, arriving=True).wait_recv()
        for b in range(nd):
            high, low = split(lf[b, xs].reshape(rows, half))
            lhi[xs, :, b * half:(b + 1) * half] = high
            llo[xs, :, b * half:(b + 1) * half] = low

    def piece_event():
        left_piece()
        depth_copy(0).start()
        for o in (1, nx - 1, 2):
            lx_copy(o, 0).start()
        y_first(x, 0)

    def lx_event(e):
        for o in (1, nx - 1, 2):
            lx_arrival(o, e).wait_recv()
            y_first(lax.rem(x + nx - o, nx), e)

    def depth_event():
        depth_copy(1).wait_recv()
        for o in (1, nx - 1, 2):
            lx_copy(o, 1).start()
        y_first(x, 1)

    def y_event(e, h):
        each_xs(lambda xs: y_later(xs, e, h))

    def own_copy(m):
        start = (base(m) + share(x, m)) * 2 * unit
        dst = out_ref.at[:, pl.ds(pl.multiple_of(start, 2 * unit), 2 * unit)]
        return pltpu.make_async_copy(obuf.at[base(m)], dst, o_own.at[m])

    def ship(m, s, to, arriving=False):
        start = (base(m) + share(to if arriving else x, m)) * 2 * unit
        dst = out_ref.at[:, pl.ds(pl.multiple_of(start, 2 * unit), 2 * unit)]
        i = base(m) + s
        return remote(obuf.at[i], dst, o_send.at[i], o_recv.at[i], dev(x=to))

    def product(i, xs):
        obuf[i] = (dot(lhi[xs], phi[...]) + dot(lhi[xs], plo[...])) + dot(llo[xs], phi[...])

    def compute(m):
        for part in range(2):
            high, low = split(gat[2 * m + part].reshape(k_full, unit))
            phi[:, part * unit:(part + 1) * unit] = high
            plo[:, part * unit:(part + 1) * unit] = low

        def send_one(s, _):
            to = jnp.where(m < wide, lax.rem(x + s, nx), partner_of(m))
            product(base(m) + s, to)
            ship(m, s, to).start()
            return 0

        lax.fori_loop(1, jnp.where(m < wide, nx, 2), send_one, 0)
        product(base(m), x)
        own_copy(m).start()

    slot(1)
    slot(2)
    piece_event()
    slot(3)
    slot(4)
    lx_event(0)
    depth_event()
    slot(5)
    lx_event(1)
    y_event(0, 2)
    slot(6)
    y_event(1, 2)
    slot(7)
    y_event(0, 3)
    slot(8)
    y_event(1, 3)
    each_xs(left_ready)

    def caught_up(m, _):
        compute(m)
        return 0

    def body(m, _):
        slot(2 * m + 5)
        slot(2 * m + 6)
        compute(m)
        return 0

    lax.fori_loop(0, min(2, pairs), caught_up, 0)
    lax.fori_loop(2, pairs, body, 0)

    def finish(j, _):
        for o in range(1, nx):
            e_copy(j, o).wait_send()
        for h in range(1, nlong + 1):
            z_copy(j, h, True).wait_send()
        for h in range(1, nshort + 1):
            z_copy(j, h, False).wait_send()
        return 0

    lax.fori_loop(0, chunks, finish, 0)

    def q_finish(o, _):
        q_copy(o).wait_send()
        return 0

    lax.fori_loop(1, nb, q_finish, 0)
    depth_copy(0).wait_send()
    for e in range(2):
        for o in range(1, nx):
            lx_copy(o, e).wait_send()

    def y_finish(xs):
        for e in range(2):
            c_copy(xs, e, 0, True).wait_send()
            for h, far in ways:
                c_copy(xs, e, h, far).wait_send()
                y_parts(xs, e, h, far, False).wait_send()

    each_xs(y_finish)

    def out_finish(m, _):
        own_copy(m).wait()

        def one(s, _):
            ship(m, s, jnp.where(m < wide, lax.rem(x + s, nx), partner_of(m))).wait_send()
            src = jnp.where(m < wide, lax.rem(x + nx - s, nx), partner_of(m))
            ship(m, s, src, arriving=True).wait_recv()
            return 0

        lax.fori_loop(1, jnp.where(m < wide, nx, 2), one, 0)
        return 0

    lax.fori_loop(0, pairs, out_finish, 0)


def per_device(dims, unit, wide, q_slab, triangle, panel_q):
    nd, ny, nc, nx, nzl = dims
    nz, nr, nb = nd * nzl, ny * nc, nd * ny * nc
    rows, qk = q_slab.shape
    k_full, half = triangle.shape
    out_cols, narrow = panel_q.shape
    blocks = out_cols // (2 * unit)
    pairs = (blocks - 4 * wide) // 2 + wide
    chunks = 2 * pairs
    dma = pltpu.SemaphoreType.DMA
    far = pl.BlockSpec(memory_space=pl.ANY)
    return pl.pallas_call(
        functools.partial(kernel, dims, unit, (wide, pairs)),
        out_shape=jax.ShapeDtypeStruct((rows, out_cols), F32),
        in_specs=[pl.BlockSpec(memory_space=pltpu.VMEM), far, far],
        out_specs=far,
        scratch_shapes=[
            pltpu.VMEM((rows, qk), F32),
            pltpu.VMEM((k_full, half), F32),
            pltpu.VMEM((narrow, out_cols), F32),
            pltpu.VMEM((nb, rows // nr, qk), F32),
            pltpu.VMEM((rows // nr, k_full), F32),
            pltpu.VMEM((nd, nx, nr, rows // nr, half), F32),
            pltpu.VMEM((nx, rows, k_full), BF16),
            pltpu.VMEM((nx, rows, k_full), BF16),
            pltpu.VMEM((chunks, nd, nx, nzl, narrow, unit), F32),
            pltpu.VMEM((k_full, 2 * unit), BF16),
            pltpu.VMEM((k_full, 2 * unit), BF16),
            pltpu.VMEM((blocks, rows, 2 * unit), F32),
            dma((2,)),
            dma((nb,)), dma((nb,)),
            dma((chunks, nx)), dma((chunks, nx)), dma((chunks,)),
            dma((chunks, nz)), dma((chunks, nz)),
            dma((1,)), dma((1,)),
            dma((nx, 2)), dma((nx, 2)),
            dma((nx, 2, ny)), dma((nx, 2, ny)),
            dma((nx, 2, ny)), dma((nx, 2, ny)),
            dma((pairs,)), dma((blocks,)), dma((blocks,)),
        ],
        compiler_params=pltpu.CompilerParams(
            collective_id=0, has_side_effects=True, vmem_limit_bytes=60 * 1024 * 1024
        ),
    )(q_slab.T, triangle, panel_q.T)


def build(mesh, dims, unit, wide=1):
    torus = Mesh(mesh.devices.reshape(dims), AXES)
    slab = ("x", "zl")
    row = ("y", "core")
    in_specs = (P(slab, ("depth",) + row), P(None, "depth"), P(row, ("depth",) + slab))
    return jax.shard_map(
        functools.partial(per_device, dims, unit, wide),
        mesh=torus, in_specs=in_specs, out_specs=P(slab, row), check_vma=False)


def solution(mesh):
    return build(mesh, (mesh.shape["depth"], 4, 2, 4, 4), 128)
```

time: 159 us -> 136 us (0.86)
  Pallas kernels: 150 us -> 129 us
  local copies, waits for them, and re-layouts: 7.9 us -> 6.2 us
    pallas_call x1, Pallas kernels: 150 us -> 129 us  [per_device(): pl.pallas_call(functools.partial(kernel, dims, unit, (wide, pairs)), out_...]
    unnamed x2 -> x1, local copies, waits for them, and re-layouts: 7.9 us -> 6.2 us
where the time goes in v2:
time: 136 us; the launch traced here: 135 us
  Pallas kernels  129 us (95%)
  local copies, waits for them, and re-layouts  6.2 us (5%)
    pallas_call x1, Pallas kernels, per_device(): pl.pallas_call(functools.partial(kernel, dims, unit, (wide, pairs)), out_...  129 us
    unnamed x1, local copies, waits for them, and re-layouts  6.2 us

profile of v2, /device:TPU:6, one launch (start us, length us, event | category | flops | bytes accessed | tf_op | source)
XLA Modules:
  0.0 135.5 jit_solution(9012280857369789287)
XLA Ops:
  0.0 129.3 %shard_map.37 = f32[384,4096]{1,0:T(8,128)} custom-call(f32[64,384]{1,0:T(8,128)} %bitcast.3, f32[1024,512]{1,0:T(8,128)} %t_hbm.1, f32[32,4096]{1,0:T(8,128)} %bitcast.2), custom_call_target="tpu_custom_call" | custom-call | tf_op jit(solution)/shard_map/pallas_call | solution.py:402
  129.3 6.2 %copy.5 = f32[384,4096]{1,0:T(8,128)} copy(f32[384,4096]{1,0:T(8,128)} %shard_map.37) | data formatting | bytes 12582912

commit v3 on v2

--- a/solution.py
+++ b/solution.py
@@ -22,12 +22,12 @@
     return jnp.dot(a, b, preferred_element_type=F32)
 
 
-def kernel(dims, unit, groups, q_ref, t_hbm, p_hbm, out_ref,
+def kernel(dims, unit, plan, q_ref, t_hbm, p_hbm, out_ref,
            qs, t_ref, p_ref, qbuf, qrow, lf, lhi, llo, gat, phi, plo, obuf, in_sem,
            q_send, q_recv, e_send, e_recv, e_own, z_send, z_recv,
            d_send, d_recv, lx_send, lx_recv, y_send, y_recv,
            c_send, c_recv, o_own, o_send, o_recv):
-    wide, pairs = groups
+    wide, pairs = plan
     nd, ny, nc, nx, nzl = dims
     nz = nd * nzl
     nr = ny * nc
@@ -37,7 +37,7 @@
     rk = y * nc + core
     me_b = d * nr + rk
     chunks = 2 * pairs
-    ahead = 6
+    ahead = 8
     piece = lf.shape[3]
     half = lf.shape[4]
     k_full = nd * half
@@ -62,13 +62,28 @@
             device_id=to, device_id_type=MESH)
 
     def base(m):
-        return 2 * m + 2 * jnp.minimum(m, wide)
+        return 2 * m + 2 * jnp.minimum(lax.div(m, 2), wide)
+
+    def is_wide(m):
+        return (lax.rem(m, 2) == 1) & (m < 2 * wide)
+
+    def role(pos, m):
+        return lax.rem(pos + lax.div(m, 2) + lax.rem(m, 2), 2)
 
     def share(pos, m):
-        return jnp.where(m < wide, pos, lax.rem(pos + m, 2))
+        return jnp.where(is_wide(m), pos, role(pos, m))
 
     def partner_of(m):
-        return lax.rem(x + 1 - 2 * lax.rem(x + m, 2) + nx, nx)
+        return lax.rem(x + 1 - 2 * role(x, m) + nx, nx)
+
+    def receivers(m):
+        return jnp.where(is_wide(m), nx - 1, 1)
+
+    def receiver(m, s):
+        return jnp.where(is_wide(m), lax.rem(x + s, nx), partner_of(m))
+
+    def sender(m, s):
+        return jnp.where(is_wide(m), lax.rem(x + nx - s, nx), partner_of(m))
 
     t_load = pltpu.make_async_copy(t_hbm, t_ref, in_sem.at[0])
     p_load = pltpu.make_async_copy(p_hbm, p_ref, in_sem.at[1])
@@ -165,19 +180,9 @@
             if h <= count:
                 z_copy(j, h, far).start()
 
-    def slot(t):
-        for h in range(nlong + 1, 0, -1):
-            if isinstance(t, int):
-                if 0 <= t - h < chunks:
-                    hop(t - h, h)
-            else:
-                pl.when((t - h >= 0) & (t - h < chunks))(functools.partial(hop, t - h, h))
-        nxt = t + ahead - 1
-        if isinstance(t, int):
-            if nxt < chunks:
-                e_start(nxt)
-        else:
-            pl.when(nxt < chunks)(functools.partial(e_start, nxt))
+    def step(g, h):
+        for c in range(4):
+            hop(4 * g + c, h)
 
     ylong, yshort = ny // 2, (ny - 1) // 2
     ways = [(h, True) for h in range(1, ylong + 1)] + [(h, False) for h in range(1, yshort + 1)]
@@ -245,12 +250,6 @@
                 if h <= count:
                     y_parts(xs, e, h, far, False).start()
                 c_copy(xs, e, h - 1, far).start()
-
-    def each_xs(work):
-        def step(o, _):
-            work(lax.rem(x + o, nx))
-            return 0
-        lax.fori_loop(0, nx, step, 0)
 
     def left_ready(xs):
         for h, far in [(0, True)] + ways:
@@ -268,19 +267,17 @@
             lx_copy(o, 0).start()
         y_first(x, 0)
 
-    def lx_event(e):
-        for o in (1, nx - 1, 2):
-            lx_arrival(o, e).wait_recv()
-            y_first(lax.rem(x + nx - o, nx), e)
+    def lx_event(o, e):
+        lx_arrival(o, e).wait_recv()
+        y_first(lax.rem(x + nx - o, nx), e)
 
     def depth_event():
         depth_copy(1).wait_recv()
         for o in (1, nx - 1, 2):
             lx_copy(o, 1).start()
-        y_first(x, 1)
-
-    def y_event(e, h):
-        each_xs(lambda xs: y_later(xs, e, h))
+
+    near = (lax.rem(x + nx - 1, nx), lax.rem(x + 1, nx))
+    across = lax.rem(x + 2, nx)
 
     def own_copy(m):
         start = (base(m) + share(x, m)) * 2 * unit
@@ -293,55 +290,91 @@
         i = base(m) + s
         return remote(obuf.at[i], dst, o_send.at[i], o_recv.at[i], dev(x=to))
 
-    def product(i, xs):
-        obuf[i] = (dot(lhi[xs], phi[...]) + dot(lhi[xs], plo[...])) + dot(llo[xs], phi[...])
-
-    def compute(m):
+    def prepare(m):
         for part in range(2):
             high, low = split(gat[2 * m + part].reshape(k_full, unit))
-            phi[:, part * unit:(part + 1) * unit] = high
-            plo[:, part * unit:(part + 1) * unit] = low
-
-        def send_one(s, _):
-            to = jnp.where(m < wide, lax.rem(x + s, nx), partner_of(m))
-            product(base(m) + s, to)
+            phi[lax.rem(m, 2), :, part * unit:(part + 1) * unit] = high
+            plo[lax.rem(m, 2), :, part * unit:(part + 1) * unit] = low
+
+    def product(m, i, xs):
+        high, low = phi[lax.rem(m, 2)], plo[lax.rem(m, 2)]
+        obuf[base(m) + i] = (dot(lhi[xs], high) + dot(lhi[xs], low)) + dot(llo[xs], high)
+
+    def compute_others(m):
+        prepare(m)
+
+        def one(s, _):
+            to = receiver(m, s)
+            product(m, s, to)
             ship(m, s, to).start()
             return 0
 
-        lax.fori_loop(1, jnp.where(m < wide, nx, 2), send_one, 0)
-        product(base(m), x)
+        lax.fori_loop(1, receivers(m) + 1, one, 0)
+
+    def compute_own(m):
+        product(m, 0, x)
         own_copy(m).start()
 
-    slot(1)
-    slot(2)
+    groups = chunks // 4
+    step(0, 1)
     piece_event()
-    slot(3)
-    slot(4)
-    lx_event(0)
+    step(0, 2)
+    for o in (1, nx - 1):
+        lx_event(o, 0)
     depth_event()
-    slot(5)
-    lx_event(1)
-    y_event(0, 2)
-    slot(6)
-    y_event(1, 2)
-    slot(7)
-    y_event(0, 3)
-    slot(8)
-    y_event(1, 3)
-    each_xs(left_ready)
-
-    def caught_up(m, _):
-        compute(m)
-        return 0
-
-    def body(m, _):
-        slot(2 * m + 5)
-        slot(2 * m + 6)
-        compute(m)
-        return 0
-
-    lax.fori_loop(0, min(2, pairs), caught_up, 0)
-    lax.fori_loop(2, pairs, body, 0)
+    step(0, 3)
+    lax.fori_loop(ahead, chunks, e_step, 0)
+    for xs in near:
+        y_later(xs, 0, 2)
+    for o in (1, nx - 1):
+        lx_event(o, 1)
+    step(0, 4)
+    step(1, 1)
+    for xs in near:
+        y_later(xs, 1, 2)
+    y_first(x, 1)
+    y_later(x, 0, 2)
+    for e in range(2):
+        lx_event(2, e)
+    step(0, 5)
+    step(1, 2)
+    for xs in near:
+        for e in range(2):
+            y_later(xs, e, 3)
+    for xs in near:
+        left_ready(xs)
+    compute_others(0)
+    y_later(x, 1, 2)
+    step(1, 3)
+    for e in range(2):
+        y_later(across, e, 2)
+        y_later(x, e, 3)
+    left_ready(x)
+    compute_own(0)
+    step(1, 4)
+    step(2, 1)
+    for e in range(2):
+        y_later(across, e, 3)
+    left_ready(across)
+    compute_others(1)
+    compute_own(1)
+    for g in range(2, groups):
+        if g > 2:
+            step(g - 1, 4)
+            step(g, 1)
+        step(g - 1, 5)
+        step(g, 2)
+        compute_others(2 * g - 2)
+        compute_own(2 * g - 2)
+        step(g, 3)
+        compute_others(2 * g - 1)
+        compute_own(2 * g - 1)
+    step(groups - 1, 4)
+    step(groups - 1, 5)
+    for m in (2 * groups - 2, 2 * groups - 1):
+        compute_others(m)
+    for m in (2 * groups - 2, 2 * groups - 1):
+        compute_own(m)
 
     def finish(j, _):
         for o in range(1, nx):
@@ -364,25 +397,25 @@
         for o in range(1, nx):
             lx_copy(o, e).wait_send()
 
-    def y_finish(xs):
+    def y_finish(xs, _):
         for e in range(2):
             c_copy(xs, e, 0, True).wait_send()
             for h, far in ways:
                 c_copy(xs, e, h, far).wait_send()
                 y_parts(xs, e, h, far, False).wait_send()
-
-    each_xs(y_finish)
+        return 0
+
+    lax.fori_loop(0, nx, y_finish, 0)
 
     def out_finish(m, _):
         own_copy(m).wait()
 
         def one(s, _):
-            ship(m, s, jnp.where(m < wide, lax.rem(x + s, nx), partner_of(m))).wait_send()
-            src = jnp.where(m < wide, lax.rem(x + nx - s, nx), partner_of(m))
-            ship(m, s, src, arriving=True).wait_recv()
+            ship(m, s, receiver(m, s)).wait_send()
+            ship(m, s, sender(m, s), arriving=True).wait_recv()
             return 0
 
-        lax.fori_loop(1, jnp.where(m < wide, nx, 2), one, 0)
+        lax.fori_loop(1, receivers(m) + 1, one, 0)
         return 0
 
     lax.fori_loop(0, pairs, out_finish, 0)
@@ -414,8 +447,8 @@
             pltpu.VMEM((nx, rows, k_full), BF16),
             pltpu.VMEM((nx, rows, k_full), BF16),
             pltpu.VMEM((chunks, nd, nx, nzl, narrow, unit), F32),
-            pltpu.VMEM((k_full, 2 * unit), BF16),
-            pltpu.VMEM((k_full, 2 * unit), BF16),
+            pltpu.VMEM((2, k_full, 2 * unit), BF16),
+            pltpu.VMEM((2, k_full, 2 * unit), BF16),
             pltpu.VMEM((blocks, rows, 2 * unit), F32),
             dma((2,)),
             dma((nb,)), dma((nb,)),
@@ -428,12 +461,12 @@
             dma((pairs,)), dma((blocks,)), dma((blocks,)),
         ],
         compiler_params=pltpu.CompilerParams(
-            collective_id=0, has_side_effects=True, vmem_limit_bytes=60 * 1024 * 1024
+            collective_id=0, has_side_effects=True, vmem_limit_bytes=57 * 1024 * 1024
         ),
     )(q_slab.T, triangle, panel_q.T)
 
 
-def build(mesh, dims, unit, wide=1):
+def build(mesh, dims, unit, wide=2):
     torus = Mesh(mesh.devices.reshape(dims), AXES)
     slab = ("x", "zl")
     row = ("y", "core")

time: 136 us -> 133 us (0.978); the launches traced: 135 us -> 131 us
  Pallas kernels: 129 us -> 125 us
    pallas_call x1, Pallas kernels: 129 us -> 125 us  [per_device(): pl.pallas_call(functools.partial(kernel, dims, unit, (wide, pairs)), out_...]
where the time goes in v3:
time: 133 us; the launch traced here: 131 us
  Pallas kernels  125 us (94%)
  local copies, waits for them, and re-layouts  6.2 us (5%)
    pallas_call x1, Pallas kernels, per_device(): pl.pallas_call(functools.partial(kernel, dims, unit, (wide, pairs)), out_...  125 us
    unnamed x1, local copies, waits for them, and re-layouts  6.2 us

profile of v3, /device:TPU:6, one launch (start us, length us, event | category | flops | bytes accessed | tf_op | source)
XLA Modules:
  0.0 131.1 jit_solution(14473907919575956918)
XLA Ops:
  0.0 124.9 %shard_map.37 = f32[384,4096]{1,0:T(8,128)} custom-call(f32[64,384]{1,0:T(8,128)} %bitcast.3, f32[1024,512]{1,0:T(8,128)} %t_hbm.1, f32[32,4096]{1,0:T(8,128)} %bitcast.2), custom_call_target="tpu_custom_call" | custom-call | tf_op jit(solution)/shard_map/pallas_call | solution.py:435
  124.9 6.2 %copy.5 = f32[384,4096]{1,0:T(8,128)} copy(f32[384,4096]{1,0:T(8,128)} %shard_map.37) | data formatting | bytes 12582912

commit v4 on v3

--- a/solution.py
+++ b/solution.py
@@ -61,14 +61,17 @@
             src_ref=src, dst_ref=dst, send_sem=send, recv_sem=recv,
             device_id=to, device_id_type=MESH)
 
+    def wide_before(m):
+        return jnp.clip(m - 2, 0, wide)
+
     def base(m):
-        return 2 * m + 2 * jnp.minimum(lax.div(m, 2), wide)
+        return 2 * m + 2 * wide_before(m)
 
     def is_wide(m):
-        return (lax.rem(m, 2) == 1) & (m < 2 * wide)
+        return (m >= 2) & (m < 2 + wide)
 
     def role(pos, m):
-        return lax.rem(pos + lax.div(m, 2) + lax.rem(m, 2), 2)
+        return lax.rem(pos + m + wide_before(m), 2)
 
     def share(pos, m):
         return jnp.where(is_wide(m), pos, role(pos, m))
@@ -181,8 +184,8 @@
                 z_copy(j, h, far).start()
 
     def step(g, h):
-        for c in range(4):
-            hop(4 * g + c, h)
+        for j in range(max(4 * g - 2, 0), 4 * g + 2):
+            hop(j, h)
 
     ylong, yshort = ny // 2, (ny - 1) // 2
     ways = [(h, True) for h in range(1, ylong + 1)] + [(h, False) for h in range(1, yshort + 1)]
@@ -293,11 +296,11 @@
     def prepare(m):
         for part in range(2):
             high, low = split(gat[2 * m + part].reshape(k_full, unit))
-            phi[lax.rem(m, 2), :, part * unit:(part + 1) * unit] = high
-            plo[lax.rem(m, 2), :, part * unit:(part + 1) * unit] = low
+            phi[lax.rem(m, 4), :, part * unit:(part + 1) * unit] = high
+            plo[lax.rem(m, 4), :, part * unit:(part + 1) * unit] = low
 
     def product(m, i, xs):
-        high, low = phi[lax.rem(m, 2)], plo[lax.rem(m, 2)]
+        high, low = phi[lax.rem(m, 4)], plo[lax.rem(m, 4)]
         obuf[base(m) + i] = (dot(lhi[xs], high) + dot(lhi[xs], low)) + dot(llo[xs], high)
 
     def compute_others(m):
@@ -315,65 +318,67 @@
         product(m, 0, x)
         own_copy(m).start()
 
-    groups = chunks // 4
     step(0, 1)
+    step(1, 1)
     piece_event()
     step(0, 2)
     for o in (1, nx - 1):
         lx_event(o, 0)
+    step(1, 2)
     depth_event()
-    step(0, 3)
     lax.fori_loop(ahead, chunks, e_step, 0)
     for xs in near:
         y_later(xs, 0, 2)
+    step(0, 3)
     for o in (1, nx - 1):
         lx_event(o, 1)
-    step(0, 4)
-    step(1, 1)
+    step(1, 3)
     for xs in near:
         y_later(xs, 1, 2)
     y_first(x, 1)
     y_later(x, 0, 2)
     for e in range(2):
         lx_event(2, e)
-    step(0, 5)
-    step(1, 2)
+    step(0, 4)
+    step(2, 1)
     for xs in near:
         for e in range(2):
             y_later(xs, e, 3)
     for xs in near:
         left_ready(xs)
+    step(1, 4)
+    step(0, 5)
     compute_others(0)
     y_later(x, 1, 2)
-    step(1, 3)
     for e in range(2):
         y_later(across, e, 2)
+    step(2, 2)
+    step(1, 5)
+    compute_others(1)
+    for e in range(2):
         y_later(x, e, 3)
+        y_later(across, e, 3)
+    step(2, 3)
+    step(3, 1)
+    left_ready(across)
+    compute_others(2)
+    step(2, 4)
+    step(3, 2)
     left_ready(x)
     compute_own(0)
-    step(1, 4)
-    step(2, 1)
-    for e in range(2):
-        y_later(across, e, 3)
-    left_ready(across)
-    compute_others(1)
     compute_own(1)
-    for g in range(2, groups):
-        if g > 2:
-            step(g - 1, 4)
-            step(g, 1)
-        step(g - 1, 5)
-        step(g, 2)
-        compute_others(2 * g - 2)
-        compute_own(2 * g - 2)
-        step(g, 3)
-        compute_others(2 * g - 1)
-        compute_own(2 * g - 1)
-    step(groups - 1, 4)
-    step(groups - 1, 5)
-    for m in (2 * groups - 2, 2 * groups - 1):
+    step(2, 5)
+    compute_others(3)
+    step(3, 3)
+    compute_others(4)
+    compute_own(2)
+    step(3, 4)
+    compute_own(3)
+    compute_own(4)
+    step(3, 5)
+    for m in range(5, pairs):
         compute_others(m)
-    for m in (2 * groups - 2, 2 * groups - 1):
+    for m in range(5, pairs):
         compute_own(m)
 
     def finish(j, _):
@@ -447,8 +452,8 @@
             pltpu.VMEM((nx, rows, k_full), BF16),
             pltpu.VMEM((nx, rows, k_full), BF16),
             pltpu.VMEM((chunks, nd, nx, nzl, narrow, unit), F32),
-            pltpu.VMEM((2, k_full, 2 * unit), BF16),
-            pltpu.VMEM((2, k_full, 2 * unit), BF16),
+            pltpu.VMEM((4, k_full, 2 * unit), BF16),
+            pltpu.VMEM((4, k_full, 2 * unit), BF16),
             pltpu.VMEM((blocks, rows, 2 * unit), F32),
             dma((2,)),
             dma((nb,)), dma((nb,)),
@@ -466,7 +471,7 @@
     )(q_slab.T, triangle, panel_q.T)
 
 
-def build(mesh, dims, unit, wide=2):
+def build(mesh, dims, unit, wide=1):
     torus = Mesh(mesh.devices.reshape(dims), AXES)
     slab = ("x", "zl")
     row = ("y", "core")

time: 133 us -> 122 us (0.917); the launches traced: 131 us -> 121 us
  Pallas kernels: 125 us -> 115 us
    pallas_call x1, Pallas kernels: 125 us -> 115 us  [per_device(): pl.pallas_call(functools.partial(kernel, dims, unit, (wide, pairs)), out_...]
where the time goes in v4:
time: 122 us; the launch traced here: 121 us
  Pallas kernels  115 us (94%)
  local copies, waits for them, and re-layouts  6.2 us (5%)
    pallas_call x1, Pallas kernels, per_device(): pl.pallas_call(functools.partial(kernel, dims, unit, (wide, pairs)), out_...  115 us
    unnamed x1, local copies, waits for them, and re-layouts  6.2 us

profile of v4, /device:TPU:6, one launch (start us, length us, event | category | flops | bytes accessed | tf_op | source)
XLA Modules:
  0.0 121.4 jit_solution(16676332483031633416)
XLA Ops:
  0.0 115.2 %shard_map.37 = f32[384,4096]{1,0:T(8,128)} custom-call(f32[64,384]{1,0:T(8,128)} %bitcast.3, f32[1024,512]{1,0:T(8,128)} %t_hbm.1, f32[32,4096]{1,0:T(8,128)} %bitcast.2), custom_call_target="tpu_custom_call" | custom-call | tf_op jit(solution)/shard_map/pallas_call | solution.py:440
  115.2 6.2 %copy.5 = f32[384,4096]{1,0:T(8,128)} copy(f32[384,4096]{1,0:T(8,128)} %shard_map.37) | data formatting | bytes 12582912

commit v5 on v4

--- a/solution.py
+++ b/solution.py
@@ -373,12 +373,11 @@
     compute_others(4)
     compute_own(2)
     step(3, 4)
-    compute_own(3)
-    compute_own(4)
-    step(3, 5)
     for m in range(5, pairs):
+        hop(2 * m, 5)
+        hop(2 * m + 1, 5)
         compute_others(m)
-    for m in range(5, pairs):
+    for m in range(3, pairs):
         compute_own(m)
 
     def finish(j, _):

time: 122 us -> 120 us (0.984)
    pallas_call x1, Pallas kernels: 115 us -> 114 us  [per_device(): pl.pallas_call(functools.partial(kernel, dims, unit, (wide, pairs)), out_...]
where the time goes in v5:
time: 120 us
  Pallas kernels  114 us (95%)
  local copies, waits for them, and re-layouts  6.2 us (5%)
    pallas_call x1, Pallas kernels, per_device(): pl.pallas_call(functools.partial(kernel, dims, unit, (wide, pairs)), out_...  114 us
    unnamed x1, local copies, waits for them, and re-layouts  6.2 us

profile of v5, /device:TPU:6, one launch (start us, length us, event | category | flops | bytes accessed | tf_op | source)
XLA Modules:
  0.0 120.0 jit_solution(15191690536680302566)
XLA Ops:
  0.0 113.8 %shard_map.37 = f32[384,4096]{1,0:T(8,128)} custom-call(f32[64,384]{1,0:T(8,128)} %bitcast.3, f32[1024,512]{1,0:T(8,128)} %t_hbm.1, f32[32,4096]{1,0:T(8,128)} %bitcast.2), custom_call_target="tpu_custom_call" | custom-call | tf_op jit(solution)/shard_map/pallas_call | solution.py:439
  113.8 6.2 %copy.5 = f32[384,4096]{1,0:T(8,128)} copy(f32[384,4096]{1,0:T(8,128)} %shard_map.37) | data formatting | bytes 12582912
